TPU v7x, 32 devices: a whole 2x2x4 slice. The times are simulated.
32 devices in a mesh: strip: 32 (over z, y, x, core).
Axes of the slice: x: 2, y: 2, z: 4, core: 2. Of those that a mesh axis runs over, the one named last changes fastest.
Arguments:
- state: float32 [4096, 4096], P('strip'), may hold values from -6 to 6
- noise: float32 [4096, 4096], P('strip'), may hold values from -6 to 6
- step: float32 [1], replicated, may hold values from 0.3 to 0.7
- field_scale: float32 [1], replicated, may hold values from 0.6 to 1.2
- wave_scale: float32 [1], replicated, may hold values from 4 to 8
- source: float32 [2048, 2048], P('strip'), may hold values from -6 to 6
- obs_cells: int32 [2048], replicated, may hold values from 0 to 4194303
- obs_values: float32 [2048], replicated, may hold values from -3 to 3
Outputs:
- log_perm: float32 [2048, 2048], P('strip')
- pressure: float32 [2048, 2048], P('strip')
- loglik: float32 [], replicated
Inputs may be any that keep to these rules, and one draw needn't show every extreme that they name: `obs_cells`: each entry is row * 2048 + column of an observed cell of the field grid.
All inputs are finite; a program needn't handle non-finite values.
Results may differ from a plain program's by a relative error of at most 0.00011.
Values sent between devices are 32-bit elements; how exact they have to be, the bound alone decides.
No kernel may reach another device: no remote copies, remote signals or barrier semaphores. Data moves between devices by JAX's collectives and lax.ppermute only.
A program may use at most 64 MiB of HBM per device.

v0:
```python
import math
import jax
import jax.numpy as jnp
from jax import lax
from jax.sharding import PartitionSpec as P

ITERS = 4
precise = lax.Precision.HIGHEST


def padded(block, sides, width):
    for axis, dim in sides:
        count = lax.axis_size(axis)
        forward = [(i, i + 1) for i in range(count - 1)]
        backward = [(target, source) for source, target in forward]
        low = lax.ppermute(
            lax.slice_in_dim(block, block.shape[dim] - width, None, axis=dim), axis, forward
        )
        high = lax.ppermute(lax.slice_in_dim(block, 0, width, axis=dim), axis, backward)
        block = jnp.concatenate([low, block, high], axis=dim)
    return block


def split_length(length):
    second = min(128, length)
    return (length // second, second)


def phase_table(height, breadth, modulus, orient):
    product = (
        lax.broadcasted_iota(jnp.int32, (height, breadth), 0)
        * lax.broadcasted_iota(jnp.int32, (height, breadth), 1)
        % modulus
    )
    angles = product.astype(jnp.float32) * (orient * 2.0 * math.pi / modulus)
    return (jnp.cos(angles), jnp.sin(angles))


def true_freq(index, factor, second):
    return index // second + factor * (index % second)


def forward_permuted(real_part, imag_part, orient):
    length = real_part.shape[-1]
    factor, second = split_length(length)
    leading = real_part.shape[:-1]
    inner_cos, inner_sin = phase_table(factor, factor, factor, orient)
    shaped = real_part.reshape(leading + (factor, second))
    section_real = jnp.einsum("kn,...na->...ka", inner_cos, shaped, precision=precise)
    section_imag = jnp.einsum("kn,...na->...ka", inner_sin, shaped, precision=precise)
    if imag_part is not None:
        shaped_imag = imag_part.reshape(leading + (factor, second))
        section_real = section_real - jnp.einsum(
            "kn,...na->...ka", inner_sin, shaped_imag, precision=precise
        )
        section_imag = section_imag + jnp.einsum(
            "kn,...na->...ka", inner_cos, shaped_imag, precision=precise
        )
    twist_cos, twist_sin = phase_table(factor, second, length, orient)
    turned_real = section_real * twist_cos - section_imag * twist_sin
    turned_imag = section_real * twist_sin + section_imag * twist_cos
    outer_cos, outer_sin = phase_table(second, second, second, orient)
    result_real = jnp.einsum(
        "ja,...ka->...kj", outer_cos, turned_real, precision=precise
    ) - jnp.einsum("ja,...ka->...kj", outer_sin, turned_imag, precision=precise)
    result_imag = jnp.einsum(
        "ja,...ka->...kj", outer_sin, turned_real, precision=precise
    ) + jnp.einsum("ja,...ka->...kj", outer_cos, turned_imag, precision=precise)
    return (result_real.reshape(leading + (length,)), result_imag.reshape(leading + (length,)))


def inverse_natural(real_part, imag_part, orient, keep, real_only=False):
    length = real_part.shape[-1]
    factor, second = split_length(length)
    leading = real_part.shape[:-1]
    shaped_real = real_part.reshape(leading + (factor, second))
    shaped_imag = imag_part.reshape(leading + (factor, second))
    inner_cos, inner_sin = phase_table(second, second, second, orient)
    section_real = jnp.einsum(
        "ak,...jk->...ja", inner_cos, shaped_real, precision=precise
    ) - jnp.einsum("ak,...jk->...ja", inner_sin, shaped_imag, precision=precise)
    section_imag = jnp.einsum(
        "ak,...jk->...ja", inner_sin, shaped_real, precision=precise
    ) + jnp.einsum("ak,...jk->...ja", inner_cos, shaped_imag, precision=precise)
    twist_cos, twist_sin = phase_table(factor, second, length, orient)
    turned_real = section_real * twist_cos - section_imag * twist_sin
    turned_imag = section_real * twist_sin + section_imag * twist_cos
    outer_cos, outer_sin = phase_table(keep // second, factor, factor, orient)
    result_real = jnp.einsum(
        "bj,...ja->...ba", outer_cos, turned_real, precision=precise
    ) - jnp.einsum("bj,...ja->...ba", outer_sin, turned_imag, precision=precise)
    result_real = result_real.reshape(leading + (keep,))
    if real_only:
        return (result_real, None)
    result_imag = jnp.einsum(
        "bj,...ja->...ba", outer_sin, turned_real, precision=precise
    ) + jnp.einsum("bj,...ja->...ba", outer_cos, turned_imag, precision=precise)
    return (result_real, result_imag.reshape(leading + (keep,)))


def amplitude(row_freq, col_freq, length, scale, wave):
    row_wave = jnp.minimum(row_freq, length - row_freq).astype(jnp.float32)
    col_wave = jnp.minimum(col_freq, length - col_freq).astype(jnp.float32)
    shape_term = 1.0 / (1.0 + (row_wave * row_wave + col_wave * col_wave) / (wave * wave))
    return scale * length / (wave * math.sqrt(math.pi)) * shape_term


def body(state, noise, step, field_scale, wave_scale, source, obs_cells, obs_values):
    parts = lax.axis_size("strip")
    position = lax.axis_index("strip")
    rows_here, length = state.shape
    half = length // 2
    factor, second = split_length(length)
    field_rows = source.shape[0]
    rate = step[0]
    sigma = field_scale[0]
    wave = wave_scale[0]
    mixed = jnp.sqrt(1.0 - rate * rate) * state + rate * noise
    row_freq = true_freq(lax.broadcasted_iota(jnp.int32, (1, length), 1), factor, second)
    width = length // parts
    freq_real, freq_imag = forward_permuted(mixed, None, -1.0)
    send_real = freq_real.reshape(rows_here, parts, width).transpose(1, 2, 0)
    send_imag = freq_imag.reshape(rows_here, parts, width).transpose(1, 2, 0)
    column_real, column_imag = (
        lax.all_to_all(send_real, "strip", split_axis=0, concat_axis=2, tiled=True),
        lax.all_to_all(send_imag, "strip", split_axis=0, concat_axis=2, tiled=True),
    )
    column_real = column_real.reshape(width, length)
    column_imag = column_imag.reshape(width, length)
    spec_real, spec_imag = forward_permuted(column_real, column_imag, -1.0)
    slot = position * width + lax.broadcasted_iota(jnp.int32, (width, 1), 0)
    col_freq = true_freq(slot, factor, second)
    scaled = amplitude(row_freq, col_freq, length, sigma, wave)
    field_real, field_imag = inverse_natural(scaled * spec_real, scaled * spec_imag, 1.0, half)
    back_real, back_imag = (
        lax.all_to_all(
            field_real.reshape(width, parts, field_rows),
            "strip",
            split_axis=1,
            concat_axis=0,
            tiled=True,
        ),
        lax.all_to_all(
            field_imag.reshape(width, parts, field_rows),
            "strip",
            split_axis=1,
            concat_axis=0,
            tiled=True,
        ),
    )
    lower_real = back_real.reshape(length, field_rows).T
    lower_imag = back_imag.reshape(length, field_rows).T
    log_perm = inverse_natural(lower_real, lower_imag, 1.0, half, True)[0] / (length * length)
    kappa = jnp.exp(log_perm)
    rimmed = padded(kappa, (("strip", 0),), 1)
    sided = jnp.pad(kappa, ((0, 0), (1, 1)))
    north = 0.5 * (kappa + rimmed[:-2])
    south = 0.5 * (kappa + rimmed[2:])
    west = 0.5 * (kappa + sided[:, :-2])
    east = 0.5 * (kappa + sided[:, 2:])
    diagonal = north + south + west + east
    pressure = jnp.zeros_like(source)
    residual = source
    direction = jnp.zeros_like(source)
    along = jnp.zeros_like(source)
    gamma_prior = jnp.float32(1.0)
    alpha_prior = jnp.float32(1.0)
    for iteration in range(ITERS):
        precond = residual / diagonal
        beside_all = padded(precond, (("strip", 0),), 1)
        beside = jnp.pad(precond, ((0, 0), (1, 1)))
        image = (
            diagonal * precond
            - north * beside_all[:-2]
            - south * beside_all[2:]
            - west * beside[:, :-2]
            - east * beside[:, 2:]
        )
        gamma, delta = lax.psum((jnp.sum(residual * precond), jnp.sum(precond * image)), "strip")
        if iteration == 0:
            alpha = gamma / delta
            direction = precond
            along = image
        else:
            ratio = gamma / gamma_prior
            alpha = gamma / (delta - ratio * gamma / alpha_prior)
            direction = precond + ratio * direction
            along = image + ratio * along
        pressure = pressure + alpha * direction
        residual = residual - alpha * along
        gamma_prior = gamma
        alpha_prior = alpha
    columns = pressure.shape[1]
    cell_row = obs_cells // columns
    cell_col = obs_cells % columns
    local_row = cell_row - position * field_rows
    inside = (local_row >= 0) & (local_row < field_rows)
    picked = pressure[jnp.clip(local_row, 0, field_rows - 1), cell_col]
    differ = jnp.where(inside, picked - obs_values, 0.0)
    total = lax.psum(jnp.sum(differ * differ), "strip")
    loglik = -(2.0 / obs_cells.shape[0]) * total
    return (log_perm, pressure, loglik)


def solution(mesh):
    placed = (P("strip", None), P("strip", None), P(), P(), P(), P("strip", None), P(), P())
    return jax.shard_map(
        body,
        mesh=mesh,
        in_specs=placed,
        out_specs=(P("strip", None), P("strip", None), P()),
        check_vma=False,
    )
```

profile of v0, /device:TPU:0, one launch (start us, length us, event | category | flops | bytes accessed | tf_op | source)
XLA Modules:
  0.0 528.5 jit_solution(12919456128651827685)
XLA Ops:
  12.2 5.2 subtract_bitcast_fusion
  17.5 7.5 %all-to-all-start = ((f32[32,128,128]{1,2,0:T(8,128)}), f32[32,128,128]{1,2,0:T(8,128)}, u32[]{:S(2)}, u32[]{:S(2)}) async-start(f32[32,128,128]{1,2,0:T(8,128)} %subtract_bitcast_fusion), calls=%async_computation | async-start | bytes 4194304 | tf_op jit(solution)/shard_map/all_to_all | solution.py:125
  24.9 5.1 fusion.20
  30.1 4.9 add_bitcast_fusion
  35.0 38.6 %all-to-all-done = f32[32,128,128]{1,2,0:T(8,128)} async-done(((f32[32,128,128]{1,2,0:T(8,128)}), f32[32,128,128]{1,2,0:T(8,128)}, u32[]{:S(2)}, u32[]{:S(2)}) %all-to-all-start) | async-done | bytes 2097184 | tf_op jit(solution)/shard_map/all_to_all | solution.py:125
  73.7 4.2 all-to-all-start.1
  88.4 38.2 %all-to-all-done.1 = f32[32,128,128]{1,2,0:T(8,128)} async-done(((f32[32,128,128]{1,2,0:T(8,128)}), f32[32,128,128]{1,2,0:T(8,128)}, u32[]{:S(2)}, u32[]{:S(2)}) %all-to-all-start.1) | async-done | bytes 2097184 | tf_op jit(solution)/shard_map/all_to_all | solution.py:126
  142.7 4.2 subtract_multiply_fusion
  167.5 4.1 all-to-all-start.2
  171.6 3.9 fusion.4
  181.6 16.3 %all-to-all-done.2 = f32[128,32,64]{0,2,1:T(8,128)S(1)} async-done(((f32[128,32,64]{0,2,1:T(8,128)}), f32[128,32,64]{0,2,1:T(8,128)S(1)}, u32[]{:S(2)}, u32[]{:S(2)}) %all-to-all-start.2) | async-done | bytes 1048608 | tf_op jit(solution)/shard_map/all_to_all | solution.py:136
  197.8 4.0 all-to-all-start.3
  205.7 22.3 %all-to-all-done.3 = f32[128,32,64]{0,2,1:T(8,128)} async-done(((f32[128,32,64]{0,2,1:T(8,128)}), f32[128,32,64]{0,2,1:T(8,128)}, u32[]{:S(2)}, u32[]{:S(2)}) %all-to-all-start.3) | async-done | bytes 1048608 | tf_op jit(solution)/shard_map/all_to_all | solution.py:143
  242.3 4.3 collective-permute-start.2
  250.8 43.0 %all-reduce.8 = (f32[]{:T(128)}, f32[]{:T(128)}) all-reduce(f32[]{:T(128)} %get-tuple-element.10, f32[]{:T(128)} %get-tuple-element.9), channel_id=1, replica_groups=mesh['strip'=32] {'strip'}, use_global_device_ids=true, to_apply=%region_1.2 | all-reduce | flops 2 | bytes 16 | tf_op jit(solution)/shard_map/psum | solution.py:179
  298.9 4.3 collective-permute-done.5
  305.1 41.9 %all-reduce.7 = (f32[]{:T(128)}, f32[]{:T(128)}) all-reduce(f32[]{:T(128)} %get-tuple-element.8, f32[]{:T(128)} %get-tuple-element.7), channel_id=1, replica_groups=mesh['strip'=32] {'strip'}, use_global_device_ids=true, to_apply=%region_5.6 | all-reduce | flops 2 | bytes 16 | tf_op jit(solution)/shard_map/psum | solution.py:179
  357.1 4.3 collective-permute-done.7
  361.4 4.3 multiply_reduce_fusion.1
  365.7 41.8 %all-reduce.6 = (f32[]{:T(128)}, f32[]{:T(128)}) all-reduce(f32[]{:T(128)} %get-tuple-element.6, f32[]{:T(128)} %get-tuple-element.5), channel_id=1, replica_groups=mesh['strip'=32] {'strip'}, use_global_device_ids=true, to_apply=%region_9.10 | all-reduce | flops 2 | bytes 16 | tf_op jit(solution)/shard_map/psum | solution.py:179
  415.9 4.2 collective-permute-done.9
  421.2 41.9 %all-reduce.5 = (f32[]{:T(128)}, f32[]{:T(128)}) all-reduce(f32[]{:T(128)} %get-tuple-element.4, f32[]{:T(128)} %get-tuple-element.3), channel_id=1, replica_groups=mesh['strip'=32] {'strip'}, use_global_device_ids=true, to_apply=%region_13.14 | all-reduce | flops 2 | bytes 16 | tf_op jit(solution)/shard_map/psum | solution.py:179
  468.8 16.6 %gather_fusion = f32[2048]{0:T(1024)S(1)} fusion(f32[64,2048]{1,0:T(8,128)S(1)} %multiply_add_fusion.1, s32[2048]{0:T(1024)S(1)} %fusion.195), kind=kCustom, calls=%fused_computation | custom fusion | bytes 32768 | tf_op jit(solution)/shard_map/gather | solution.py:198
  486.1 40.2 %psum.71 = f32[]{:T(128)} all-reduce(f32[]{:T(128)} %multiply_reduce_fusion.7), channel_id=1, replica_groups=mesh['strip'=32] {'strip'}, use_global_device_ids=true, to_apply=%region_17.18 | all-reduce | flops 1 | bytes 8 | tf_op jit(solution)/shard_map/psum | solution.py:200
  (93 shorter events, 103.6 us)
Async XLA Ops:
  8.6 3.6 copy-start.2
  17.5 56.2 %all-to-all-start = ((f32[32,128,128]{1,2,0:T(8,128)}), f32[32,128,128]{1,2,0:T(8,128)}, u32[]{:S(2)}, u32[]{:S(2)}) async-start(f32[32,128,128]{1,2,0:T(8,128)} %subtract_bitcast_fusion), calls=%async_computation | async-start | bytes 4194304 | tf_op jit(solution)/shard_map/all_to_all | solution.py:125
  73.7 52.9 %all-to-all-start.1 = ((f32[32,128,128]{1,2,0:T(8,128)}), f32[32,128,128]{1,2,0:T(8,128)}, u32[]{:S(2)}, u32[]{:S(2)}) async-start(f32[32,128,128]{1,2,0:T(8,128)} %add_bitcast_fusion), calls=%async_computation.1 | async-start | bytes 4194304 | tf_op jit(solution)/shard_map/all_to_all | solution.py:126
  129.2 3.8 copy-start.3
  159.9 1.3 copy-start.1
  167.5 30.3 %all-to-all-start.2 = ((f32[128,32,64]{0,2,1:T(8,128)}), f32[128,32,64]{0,2,1:T(8,128)S(1)}, u32[]{:S(2)}, u32[]{:S(2)}) async-start(f32[128,32,64]{0,2,1:T(8,128)} %bitcast.183), calls=%async_computation.2 | async-start | bytes 2097152 | tf_op jit(solution)/shard_map/all_to_all | solution.py:136
  197.8 30.1 %all-to-all-start.3 = ((f32[128,32,64]{0,2,1:T(8,128)}), f32[128,32,64]{0,2,1:T(8,128)}, u32[]{:S(2)}, u32[]{:S(2)}) async-start(f32[128,32,64]{0,2,1:T(8,128)} %bitcast.33), calls=%async_computation.3 | async-start | bytes 2097152 | tf_op jit(solution)/shard_map/all_to_all | solution.py:143
  233.9 7.9 %copy-start.7 = (f32[64,2048]{1,0:T(8,128)S(1)}, f32[64,2048]{1,0:T(8,128)}, u32[]{:S(2)}) copy-start(f32[64,2048]{1,0:T(8,128)} %param.13) | copy-start | bytes 1572868
  235.8 2.6 collective-permute-start
  237.1 4.8 collective-permute-start.1
  242.3 5.6 %collective-permute-start.2 = (f32[1,2048]{1,0:T(1,128)S(1)}, f32[1,2048]{1,0:T(1,128)S(1)}, u32[]{:S(2)}, u32[]{:S(2)}) collective-permute-start(f32[1,2048]{1,0:T(1,128)S(1)} %get-tuple-element.46), channel_id=1, source_target_pairs={{0,1},{1,2},{2,3},{3,4},{4,5},{5,6},{6,7},{7,8},{8,9},{9,10},{10,1... | collective-permute-start | bytes 24584 | tf_op jit(solution)/shard_map/ppermute | solution.py:16
  246.6 3.1 collective-permute-start.3
  296.2 6.9 %copy-start.4 = (f32[64,2048]{1,0:T(8,128)}, f32[64,2048]{1,0:T(8,128)S(1)}, u32[]{:S(2)}) copy-start(f32[64,2048]{1,0:T(8,128)S(1)} %get-tuple-element.25) | copy-start | bytes 1572868
  296.2 8.9 %copy-start.8 = (f32[64,2048]{1,0:T(8,128)}, f32[64,2048]{1,0:T(8,128)S(1)}, u32[]{:S(2)}) copy-start(f32[64,2048]{1,0:T(8,128)S(1)} %get-tuple-element.26) | copy-start | bytes 1572868
  296.2 2.6 collective-permute-start.4
  297.5 5.6 %collective-permute-start.5 = (f32[1,2048]{1,0:T(1,128)S(1)}, f32[1,2048]{1,0:T(1,128)S(1)}, u32[]{:S(2)}, u32[]{:S(2)}) collective-permute-start(f32[1,2048]{1,0:T(1,128)S(1)} %get-tuple-element.45), channel_id=1, source_target_pairs={{1,0},{2,1},{3,2},{4,3},{5,4},{6,5},{7,6},{8,7},{9,8},{10,9},{11,1... | collective-permute-start | bytes 24584 | tf_op jit(solution)/shard_map/ppermute | solution.py:19
  354.5 2.6 collective-permute-start.6
  355.8 5.6 %collective-permute-start.7 = (f32[1,2048]{1,0:T(1,128)S(1)}, f32[1,2048]{1,0:T(1,128)S(1)}, u32[]{:S(2)}, u32[]{:S(2)}) collective-permute-start(f32[1,2048]{1,0:T(1,128)S(1)} %get-tuple-element.43), channel_id=1, source_target_pairs={{1,0},{2,1},{3,2},{4,3},{5,4},{6,5},{7,6},{8,7},{9,8},{10,9},{11,1... | collective-permute-start | bytes 24584 | tf_op jit(solution)/shard_map/ppermute | solution.py:19
  365.7 50.1 %copy-start.9 = (s32[2048]{0:T(1024)S(1)}, s32[2048]{0:T(1024)}, u32[]{:S(2)}) copy-start(s32[2048]{0:T(1024)} %param.14) | copy-start | bytes 24580
  413.2 8.0 %copy-start.6 = (f32[64,2048]{1,0:T(8,128)}, f32[64,2048]{1,0:T(8,128)S(1)}, u32[]{:S(2)}) copy-start(f32[64,2048]{1,0:T(8,128)S(1)} %get-tuple-element.19) | copy-start | bytes 1572868
  413.2 2.6 collective-permute-start.8
  414.5 5.6 %collective-permute-start.9 = (f32[1,2048]{1,0:T(1,128)S(1)}, f32[1,2048]{1,0:T(1,128)S(1)}, u32[]{:S(2)}, u32[]{:S(2)}) collective-permute-start(f32[1,2048]{1,0:T(1,128)S(1)} %get-tuple-element.41), channel_id=1, source_target_pairs={{1,0},{2,1},{3,2},{4,3},{5,4},{6,5},{7,6},{8,7},{9,8},{10,9},{11,1... | collective-permute-start | bytes 24584 | tf_op jit(solution)/shard_map/ppermute | solution.py:19
  468.7 16.7 %copy-start = (f32[64,2048]{1,0:T(8,128)}, f32[64,2048]{1,0:T(8,128)S(1)}, u32[]{:S(2)}) copy-start(f32[64,2048]{1,0:T(8,128)S(1)} %multiply_add_fusion.1) | copy-start | bytes 1572868
  468.8 16.7 %copy-start.10 = (f32[2048]{0:T(1024)S(1)}, f32[2048]{0:T(1024)}, u32[]{:S(2)}) copy-start(f32[2048]{0:T(1024)} %param.15) | copy-start | bytes 24580
  (1 other events, 0.8 us)
where the time goes:
time: 539 us; the launch traced here: 528 us
  blocking collectives  209 us (39%)
  waiting for transfers between devices  133 us (25%)
  matrix products  79.3 us (15%)
  starting transfers between devices  35.6 us (7%)
  local copies, waits for them, and re-layouts  33.2 us (6%)
  between operations  19.5 us (4%)
  other arithmetic  18.7 us (3%)
    psum x4, blocking collectives, body(): lax.psum((jnp.sum(residual * precond), jnp.sum(precond * image)), 'strip')  169 us
    psum x1, blocking collectives, body(): total = lax.psum(jnp.sum(differ * differ), 'strip')  40.2 us
    all_to_all x1, waiting for transfers between devices, body(): lax.all_to_all(send_real, 'strip', split_axis=0, concat_axis=2, tiled=True)  38.6 us
    all_to_all x1, waiting for transfers between devices, body(): lax.all_to_all(send_imag, 'strip', split_axis=0, concat_axis=2, tiled=True)  38.2 us
    all_to_all x1, waiting for transfers between devices, body(): lax.all_to_all(field_imag.reshape(width, parts, field_rows), 'strip', spl...  22.3 us
    ppermute x5, waiting for transfers between devices, padded(): lax.ppermute(lax.slice_in_dim(block, 0, width, axis=dim), axis, backward)  18 us
    gather x1, local copies, waits for them, and re-layouts, body(): picked = pressure[jnp.clip(local_row, 0, field_rows - 1), cell_col]  16.6 us
    all_to_all x1, waiting for transfers between devices, body(): lax.all_to_all(field_real.reshape(width, parts, field_rows), 'strip', spl...  16.3 us
  transfers between devices with their start and end apart: 14, of which 9 were waited for; matrix products, arithmetic and copies ran while one was open for 6% of the time, Pallas kernels for 0%

commit v1 on v0

--- a/solution.py
+++ b/solution.py
@@ -140,12 +140,18 @@
             concat_axis=0,
             tiled=True,
         ),
-        lax.all_to_all(
-            field_imag.reshape(width, parts, field_rows),
-            "strip",
-            split_axis=1,
-            concat_axis=0,
-            tiled=True,
+        jnp.concatenate(
+            lax.all_to_all(
+                jnp.stack(
+                    jnp.split(
+                        field_imag.reshape(width, parts, field_rows), lax.axis_size("strip"), axis=1
+                    )
+                ),
+                "strip",
+                0,
+                0,
+            ),
+            axis=0,
         ),
     )
     lower_real = back_real.reshape(length, field_rows).T

time: 539 us -> 560 us (1.039)
  local copies, waits for them, and re-layouts: 33.2 us -> 50.8 us
    unnamed x27 -> x58, local copies, waits for them, and re-layouts: 4.11 us -> 21.8 us
  transfers between devices with their start and end apart: 14 -> 14, of which waited for: 9 -> 9; matrix products, arithmetic and copies ran while one was open for 6% -> 5% of each run, Pallas kernels for 0% -> 0%
where the time goes in v1:
time: 560 us; the launch traced here: 550 us
  blocking collectives  209 us (37%)
  waiting for transfers between devices  137 us (24%)
  matrix products  79.6 us (14%)
  local copies, waits for them, and re-layouts  50.8 us (9%)
  starting transfers between devices  35.3 us (6%)
  between operations  19.2 us (3%)
  other arithmetic  18.7 us (3%)
    psum x4, blocking collectives, body(): lax.psum((jnp.sum(residual * precond), jnp.sum(precond * image)), 'strip')  169 us
    psum x1, blocking collectives, body(): total = lax.psum(jnp.sum(differ * differ), 'strip')  40.2 us
    all_to_all x1, waiting for transfers between devices, body(): lax.all_to_all(send_real, 'strip', split_axis=0, concat_axis=2, tiled=True)  38.6 us
    all_to_all x1, waiting for transfers between devices, body(): lax.all_to_all(send_imag, 'strip', split_axis=0, concat_axis=2, tiled=True)  38.2 us
    all_to_all x1, waiting for transfers between devices, body(): lax.all_to_all(jnp.stack(jnp.split(field_imag.reshape(width, parts, field...  22.3 us
    unnamed x58, local copies, waits for them, and re-layouts  21.8 us
    all_to_all x1, waiting for transfers between devices, body(): lax.all_to_all(field_real.reshape(width, parts, field_rows), 'strip', spl...  20.1 us
    ppermute x5, waiting for transfers between devices, padded(): lax.ppermute(lax.slice_in_dim(block, 0, width, axis=dim), axis, backward)  18 us
  transfers between devices with their start and end apart: 14, of which 9 were waited for; matrix products, arithmetic and copies ran while one was open for 5% of the time, Pallas kernels for 0%

profile of v1, /device:TPU:0, one launch (start us, length us, event | category | flops | bytes accessed | tf_op | source)
XLA Modules:
  0.0 549.5 jit_solution(11513130941605076728)
XLA Ops:
  12.2 5.1 subtract_bitcast_fusion
  17.3 7.5 %all-to-all-start = ((f32[32,128,128]{1,2,0:T(8,128)}), f32[32,128,128]{1,2,0:T(8,128)}, u32[]{:S(2)}, u32[]{:S(2)}) async-start(f32[32,128,128]{1,2,0:T(8,128)} %subtract_bitcast_fusion), calls=%async_computation | async-start | bytes 4194304 | tf_op jit(solution)/shard_map/all_to_all | solution.py:125
  24.8 5.1 fusion.20
  29.9 4.9 add_bitcast_fusion
  34.8 38.6 %all-to-all-done = f32[32,128,128]{1,2,0:T(8,128)} async-done(((f32[32,128,128]{1,2,0:T(8,128)}), f32[32,128,128]{1,2,0:T(8,128)}, u32[]{:S(2)}, u32[]{:S(2)}) %all-to-all-start) | async-done | bytes 2097184 | tf_op jit(solution)/shard_map/all_to_all | solution.py:125
  73.5 4.2 all-to-all-start.1
  88.2 38.2 %all-to-all-done.1 = f32[32,128,128]{1,2,0:T(8,128)} async-done(((f32[32,128,128]{1,2,0:T(8,128)}), f32[32,128,128]{1,2,0:T(8,128)}, u32[]{:S(2)}, u32[]{:S(2)}) %all-to-all-start.1) | async-done | bytes 2097184 | tf_op jit(solution)/shard_map/all_to_all | solution.py:126
  129.2 3.8 convolution_subtract_fusion
  142.8 4.0 subtract_multiply_fusion
  151.1 3.9 add_multiply_fusion
  190.4 4.1 all-to-all-start.2
  200.6 20.1 %all-to-all-done.2 = f32[128,32,64]{0,2,1:T(8,128)S(1)} async-done(((f32[128,32,64]{0,2,1:T(8,128)}), f32[128,32,64]{0,2,1:T(8,128)S(1)}, u32[]{:S(2)}, u32[]{:S(2)}) %all-to-all-start.2) | async-done | bytes 1048608 | tf_op jit(solution)/shard_map/all_to_all | solution.py:136
  228.2 22.3 %all-to-all-done.3 = f32[32,128,1,64]{1,3,2,0:T(8,128)S(1)} async-done(((f32[32,128,1,64]{1,3,2,0:T(8,128)}), f32[32,128,1,64]{1,3,2,0:T(8,128)S(1)}, u32[]{:S(2)}, u32[]{:S(2)}) %all-to-all-start.3) | async-done | bytes 1048608 | tf_op jit(solution)/shard_map/all_to_all | solution.py:144
  263.6 4.3 collective-permute-start.2
  272.1 43.0 %all-reduce.8 = (f32[]{:T(128)}, f32[]{:T(128)}) all-reduce(f32[]{:T(128)} %get-tuple-element.10, f32[]{:T(128)} %get-tuple-element.9), channel_id=1, replica_groups=mesh['strip'=32] {'strip'}, use_global_device_ids=true, to_apply=%region_1.2 | all-reduce | flops 2 | bytes 16 | tf_op jit(solution)/shard_map/psum | solution.py:185
  320.2 4.3 collective-permute-done.5
  326.4 41.8 %all-reduce.7 = (f32[]{:T(128)}, f32[]{:T(128)}) all-reduce(f32[]{:T(128)} %get-tuple-element.8, f32[]{:T(128)} %get-tuple-element.7), channel_id=1, replica_groups=mesh['strip'=32] {'strip'}, use_global_device_ids=true, to_apply=%region_5.6 | all-reduce | flops 2 | bytes 16 | tf_op jit(solution)/shard_map/psum | solution.py:185
  378.4 4.3 collective-permute-done.7
  382.7 4.3 multiply_reduce_fusion.1
  387.0 41.8 %all-reduce.6 = (f32[]{:T(128)}, f32[]{:T(128)}) all-reduce(f32[]{:T(128)} %get-tuple-element.6, f32[]{:T(128)} %get-tuple-element.5), channel_id=1, replica_groups=mesh['strip'=32] {'strip'}, use_global_device_ids=true, to_apply=%region_9.10 | all-reduce | flops 2 | bytes 16 | tf_op jit(solution)/shard_map/psum | solution.py:185
  437.2 4.2 collective-permute-done.9
  442.5 41.9 %all-reduce.5 = (f32[]{:T(128)}, f32[]{:T(128)}) all-reduce(f32[]{:T(128)} %get-tuple-element.4, f32[]{:T(128)} %get-tuple-element.3), channel_id=1, replica_groups=mesh['strip'=32] {'strip'}, use_global_device_ids=true, to_apply=%region_13.14 | all-reduce | flops 2 | bytes 16 | tf_op jit(solution)/shard_map/psum | solution.py:185
  490.1 16.6 %gather_fusion = f32[2048]{0:T(1024)S(1)} fusion(f32[64,2048]{1,0:T(8,128)S(1)} %multiply_add_fusion.1, s32[2048]{0:T(1024)S(1)} %fusion.195), kind=kCustom, calls=%fused_computation | custom fusion | bytes 32768 | tf_op jit(solution)/shard_map/gather | solution.py:204
  507.4 40.2 %psum.71 = f32[]{:T(128)} all-reduce(f32[]{:T(128)} %multiply_reduce_fusion.7), channel_id=1, replica_groups=mesh['strip'=32] {'strip'}, use_global_device_ids=true, to_apply=%region_17.18 | all-reduce | flops 1 | bytes 8 | tf_op jit(solution)/shard_map/psum | solution.py:206
  (125 shorter events, 121.6 us)
Async XLA Ops:
  8.6 3.6 copy-start.1
  17.3 56.2 %all-to-all-start = ((f32[32,128,128]{1,2,0:T(8,128)}), f32[32,128,128]{1,2,0:T(8,128)}, u32[]{:S(2)}, u32[]{:S(2)}) async-start(f32[32,128,128]{1,2,0:T(8,128)} %subtract_bitcast_fusion), calls=%async_computation | async-start | bytes 4194304 | tf_op jit(solution)/shard_map/all_to_all | solution.py:125
  73.5 52.9 %all-to-all-start.1 = ((f32[32,128,128]{1,2,0:T(8,128)}), f32[32,128,128]{1,2,0:T(8,128)}, u32[]{:S(2)}, u32[]{:S(2)}) async-start(f32[32,128,128]{1,2,0:T(8,128)} %add_bitcast_fusion), calls=%async_computation.1 | async-start | bytes 4194304 | tf_op jit(solution)/shard_map/all_to_all | solution.py:126
  129.2 3.8 copy-start.2
  170.9 13.5 %copy-start.8 = (f32[128,128,16]{1,2,0:T(8,128)S(1)}, f32[128,128,16]{1,2,0:T(8,128)}, u32[]{:S(2)}) copy-start(f32[128,128,16]{1,2,0:T(8,128)} %fusion.6) | copy-start | bytes 3145732
  190.4 30.3 %all-to-all-start.2 = ((f32[128,32,64]{0,2,1:T(8,128)}), f32[128,32,64]{0,2,1:T(8,128)S(1)}, u32[]{:S(2)}, u32[]{:S(2)}) async-start(f32[128,32,64]{0,2,1:T(8,128)} %bitcast.28), calls=%async_computation.2 | async-start | bytes 2097152 | tf_op jit(solution)/shard_map/all_to_all | solution.py:136
  220.7 29.8 %all-to-all-start.3 = ((f32[32,128,1,64]{1,3,2,0:T(8,128)}), f32[32,128,1,64]{1,3,2,0:T(8,128)S(1)}, u32[]{:S(2)}, u32[]{:S(2)}) async-start(f32[32,128,1,64]{1,3,2,0:T(8,128)} %constant_dynamic-update-slice_fusion), calls=%async_computation.3 | async-start | bytes 2097152 | tf_op jit(solution)/shard_map/all_to_all | solution.py:144
  255.3 7.9 %copy-start.6 = (f32[64,2048]{1,0:T(8,128)S(1)}, f32[64,2048]{1,0:T(8,128)}, u32[]{:S(2)}) copy-start(f32[64,2048]{1,0:T(8,128)} %param.13) | copy-start | bytes 1572868
  257.1 2.6 collective-permute-start
  258.4 4.8 collective-permute-start.1
  263.6 5.6 %collective-permute-start.2 = (f32[1,2048]{1,0:T(1,128)S(1)}, f32[1,2048]{1,0:T(1,128)S(1)}, u32[]{:S(2)}, u32[]{:S(2)}) collective-permute-start(f32[1,2048]{1,0:T(1,128)S(1)} %get-tuple-element.46), channel_id=1, source_target_pairs={{0,1},{1,2},{2,3},{3,4},{4,5},{5,6},{6,7},{7,8},{8,9},{9,10},{10,1... | collective-permute-start | bytes 24584 | tf_op jit(solution)/shard_map/ppermute | solution.py:16
  268.0 3.1 collective-permute-start.3
  317.5 6.9 %copy-start.3 = (f32[64,2048]{1,0:T(8,128)}, f32[64,2048]{1,0:T(8,128)S(1)}, u32[]{:S(2)}) copy-start(f32[64,2048]{1,0:T(8,128)S(1)} %get-tuple-element.25) | copy-start | bytes 1572868
  317.5 8.9 %copy-start.7 = (f32[64,2048]{1,0:T(8,128)}, f32[64,2048]{1,0:T(8,128)S(1)}, u32[]{:S(2)}) copy-start(f32[64,2048]{1,0:T(8,128)S(1)} %get-tuple-element.26) | copy-start | bytes 1572868
  317.6 2.6 collective-permute-start.4
  318.9 5.6 %collective-permute-start.5 = (f32[1,2048]{1,0:T(1,128)S(1)}, f32[1,2048]{1,0:T(1,128)S(1)}, u32[]{:S(2)}, u32[]{:S(2)}) collective-permute-start(f32[1,2048]{1,0:T(1,128)S(1)} %get-tuple-element.45), channel_id=1, source_target_pairs={{1,0},{2,1},{3,2},{4,3},{5,4},{6,5},{7,6},{8,7},{9,8},{10,9},{11,1... | collective-permute-start | bytes 24584 | tf_op jit(solution)/shard_map/ppermute | solution.py:19
  375.8 2.6 collective-permute-start.6
  377.1 5.6 %collective-permute-start.7 = (f32[1,2048]{1,0:T(1,128)S(1)}, f32[1,2048]{1,0:T(1,128)S(1)}, u32[]{:S(2)}, u32[]{:S(2)}) collective-permute-start(f32[1,2048]{1,0:T(1,128)S(1)} %get-tuple-element.43), channel_id=1, source_target_pairs={{1,0},{2,1},{3,2},{4,3},{5,4},{6,5},{7,6},{8,7},{9,8},{10,9},{11,1... | collective-permute-start | bytes 24584 | tf_op jit(solution)/shard_map/ppermute | solution.py:19
  387.0 50.1 %copy-start.9 = (s32[2048]{0:T(1024)S(1)}, s32[2048]{0:T(1024)}, u32[]{:S(2)}) copy-start(s32[2048]{0:T(1024)} %param.14) | copy-start | bytes 24580
  434.5 8.0 %copy-start.5 = (f32[64,2048]{1,0:T(8,128)}, f32[64,2048]{1,0:T(8,128)S(1)}, u32[]{:S(2)}) copy-start(f32[64,2048]{1,0:T(8,128)S(1)} %get-tuple-element.19) | copy-start | bytes 1572868
  434.5 2.6 collective-permute-start.8
  435.8 5.6 %collective-permute-start.9 = (f32[1,2048]{1,0:T(1,128)S(1)}, f32[1,2048]{1,0:T(1,128)S(1)}, u32[]{:S(2)}, u32[]{:S(2)}) collective-permute-start(f32[1,2048]{1,0:T(1,128)S(1)} %get-tuple-element.41), channel_id=1, source_target_pairs={{1,0},{2,1},{3,2},{4,3},{5,4},{6,5},{7,6},{8,7},{9,8},{10,9},{11,1... | collective-permute-start | bytes 24584 | tf_op jit(solution)/shard_map/ppermute | solution.py:19
  490.0 16.7 %copy-start = (f32[64,2048]{1,0:T(8,128)}, f32[64,2048]{1,0:T(8,128)S(1)}, u32[]{:S(2)}) copy-start(f32[64,2048]{1,0:T(8,128)S(1)} %multiply_add_fusion.1) | copy-start | bytes 1572868
  490.1 16.7 %copy-start.10 = (f32[2048]{0:T(1024)S(1)}, f32[2048]{0:T(1024)}, u32[]{:S(2)}) copy-start(f32[2048]{0:T(1024)} %param.15) | copy-start | bytes 24580
  (1 other events, 0.8 us)
